TPU v7x, 32 devices: a whole 2x2x4 slice. The times are simulated.
32 devices in a mesh: pair: 4 (over y, x), grow: 4 (over z), gcol: 2 (over core).
Axes of the slice: x: 2, y: 2, z: 4, core: 2. Of those that a mesh axis runs over, the one named last changes fastest.
Arguments:
- valence: bfloat16 [16, 96, 9216], P(None, 'grow'), may hold values from -6 to 6
- conduction: bfloat16 [16, 96, 9216], P(('pair', 'gcol'), 'grow'), may hold values from -6 to 6
- val_energy: float32 [16], replicated, may hold values from -10 to -1
- cond_energy: float32 [16], replicated, may hold values from 1 to 20
- val_occupation: int32 [16], replicated, may hold values from 1 to 16
- gvectors: int32 [3, 3840], replicated, may hold values from -12 to 12, as said below
Outputs:
- chi_zero: float32 [7680, 7680], P(('pair', 'gcol'), 'grow')
Inputs may be any that keep to these rules, and one draw needn't show every extreme that they name: gvectors holds 3840 distinct wave vectors; the first component lies in 1 .. 12, the other two in -12 .. 12.
All inputs are finite; a program needn't handle non-finite values.
Results may differ from a plain program's by a relative error of at most 0.02.
Values may be sent and summed in bfloat16 or wider, within the bound.
A program may use at most 128 MiB of HBM per device.

v0:
```python
import functools
import math

import jax
import jax.numpy as jnp
import numpy as np
from jax import lax
from jax.experimental import pallas as pl
from jax.experimental.pallas import tpu as pltpu
from jax.sharding import PartitionSpec as P

N = 96
RAD = 12
KG = 3840
NV = 16


def wave_tables(positions, frequencies):
    phases = jnp.mod(positions[:, None] * frequencies[None, :], N).astype(jnp.float32) * (
        2.0 * math.pi / N
    )
    return (jnp.cos(phases), jnp.sin(phases))


def build_tables(x_positions):
    all_freq = jnp.arange(-RAD, RAD + 1, dtype=jnp.int32)
    pos_freq = jnp.arange(1, RAD + 1, dtype=jnp.int32)
    positions = jnp.arange(N, dtype=jnp.int32)
    cosine, sine_part = wave_tables(positions, all_freq)
    z_table = jnp.concatenate([cosine, sine_part], 1).astype(jnp.bfloat16)
    y_table = jnp.stack(
        [jnp.stack([cosine, sine_part], 1), jnp.stack([-sine_part, cosine], 1)], 1
    ).astype(jnp.bfloat16)
    x_cos, x_sin = wave_tables(x_positions, pos_freq)
    x_table = jnp.stack([jnp.stack([x_cos, -x_sin], 1), jnp.stack([-x_sin, -x_cos], 1)], 1).astype(
        jnp.bfloat16
    )
    return (z_table, y_table, x_table)


def pair_product(left_rows, right_rows):
    return lax.dot_general(
        left_rows, right_rows, (((0,), (0,)), ((), ())), preferred_element_type=jnp.float32
    )


def body(valence, conduction, val_energy, cond_energy, val_occupation, gvectors):
    pair_count = lax.axis_size("pair")
    gcol_count = lax.axis_size("gcol")
    planes = valence.shape[1]
    cond_bands = conduction.shape[0]
    extent = 2 * RAD + 1
    local_pairs = cond_bands * NV
    x_positions = lax.axis_index("grow") * planes + jnp.arange(planes, dtype=jnp.int32)
    z_table, y_table, x_table = build_tables(x_positions)
    flat_index = ((gvectors[0] - 1) * extent + gvectors[1] + RAD) * extent + gvectors[2] + RAD
    density = conduction[:, None] * valence[None]
    section_one = jnp.dot(
        density.reshape(-1, N), z_table, preferred_element_type=jnp.float32
    ).astype(jnp.bfloat16)
    section_one = section_one.reshape(local_pairs * planes, N, 2, extent)
    second = jnp.einsum(
        "ayik,yioj->aojk", section_one, y_table, preferred_element_type=jnp.float32
    ).astype(jnp.bfloat16)
    second = second.reshape(local_pairs, planes, 2, extent * extent)
    section_three = jnp.einsum(
        "pxoq,xosm->psmq", second, x_table, preferred_element_type=jnp.float32
    )
    section_three = section_three.reshape(local_pairs, 2, RAD * extent * extent)
    picked = jnp.take(section_three, flat_index, axis=2).reshape(local_pairs, 2 * KG)
    summed = lax.psum_scatter(
        picked.astype(jnp.bfloat16), "grow", scatter_dimension=1, tiled=True
    ).astype(jnp.float32)
    first_band = (lax.axis_index("pair") * gcol_count + lax.axis_index("gcol")) * cond_bands
    own_energy = lax.dynamic_slice_in_dim(cond_energy, first_band, cond_bands, 0)
    weight = val_occupation.astype(jnp.float32)[None, :] / (
        4.0 * (own_energy[:, None] - val_energy[None, :])
    )
    factor = (jnp.sqrt(weight) * (1.0 / N**1.5)).reshape(local_pairs, 1)
    weighted = (summed * factor).astype(jnp.bfloat16)
    prefactor = -1.0 / math.sqrt(pair_count * gcol_count * local_pairs)
    full_rows = lax.all_gather(weighted, "grow", axis=1, tiled=True)
    row_part = lax.all_to_all(full_rows, "pair", split_axis=1, concat_axis=0, tiled=True)
    partial_value = pair_product(row_part, lax.all_gather(weighted, "pair", axis=0, tiled=True))
    return lax.psum_scatter(
        (partial_value * prefactor).astype(jnp.bfloat16), "gcol", scatter_dimension=0, tiled=True
    ).astype(jnp.float32)


EXT = 2 * RAD + 1
QUARTER = N * N // 4
STEP = 8 * N
CLASSES = ((0, 4, 8, 12), (2, 6, 10), (1, 3, 5, 7, 9, 11))
WIDTHS = (128, 128, 256)
ROWS = (104, 80, 152)
STARTS = (0, 104, 184)
NR = 336


def half_plane_tables():
    total = 2 * sum(WIDTHS)
    left = np.zeros((2, N // 4, total), np.float32)
    right = np.zeros((2, N, total), np.float32)
    sign = np.zeros((1, WIDTHS[2]), np.float32)
    y = np.arange(N // 4)[:, None]
    z = np.arange(N)[:, None]
    k = np.arange(-RAD, RAD + 1)
    base = 0
    for freqs, width in zip(CLASSES, WIDTHS):
        jj = np.repeat(np.array(freqs), EXT)[None]
        kk = np.tile(k, len(freqs))[None]
        count = jj.shape[1]
        ay = 2 * np.pi * ((jj * y) % N) / N
        az = 2 * np.pi * ((kk * z) % N) / N
        for part in range(2):
            cols = slice(base + part * width, base + part * width + count)
            left[0, :, cols] = np.sin(ay) if part else np.cos(ay)
            left[1, :, cols] = np.cos(ay) if part else -np.sin(ay)
            right[0, :, cols] = np.cos(az)
            right[1, :, cols] = np.sin(az)
        base += 2 * width
    jj = np.repeat(np.array(CLASSES[2]), EXT)
    sign[0, : jj.size] = np.where(jj % 4 == 1, 1.0, -1.0)
    return left, right, sign


def plane_table(pairs):
    x = np.arange(N)[:, None]
    a = np.arange(1, RAD + 1)[None]
    ang = 2 * np.pi * ((a * x) % N) / N
    c, s = np.cos(ang), np.sin(ang)
    tab = np.stack([np.stack([c, -s, c, -s], -1), np.stack([-s, -c, s, c], -1)])
    return np.repeat(tab.reshape(2, N, RAD * 4), pairs, axis=2).astype(np.float32)


def row_index(a, b, d):
    flip = b < 0
    j = jnp.abs(b)
    k = jnp.where(flip, -d, d) + RAD
    row = jnp.where(
        (j & 1) == 1,
        STARTS[2] + (j >> 1) * EXT,
        jnp.where((j & 3) == 2, STARTS[1], STARTS[0]) + (j >> 2) * EXT,
    )
    return jnp.maximum((jnp.where(flip, RAD, 0) + a - 1) * NR + row + k, 0)


def chi_kernel(
    occ, val_e, cond_e, gvec, v0, v1, v2, v3, c0, c1, c2, c3, left, right, sign, xtab,
    cols_out, rows_out,
    ee, eo, oo, tabs, acc_ee, acc_eo, acc_o, xmat, sec, got, part, inbox, blocks, cols, rows,
    index, idx, sends, recvs, outs,
):
    band, step = pl.program_id(0), pl.program_id(1)
    bands, steps = part.shape[0], tabs.shape[0]
    nv, planes, _ = v0.shape
    height = nv * planes
    lanes = 128
    per_tile = lanes // (4 * nv)
    f32, bf16 = jnp.float32, jnp.bfloat16
    _, count, _, width = blocks.shape
    n = count - 1
    p, g, c = lax.axis_index("pair"), lax.axis_index("grow"), lax.axis_index("gcol")
    me = p * 2 + c
    turn = lambda at, k: lax.rem(at + k, count)
    block = lambda at: pl.ds(pl.multiple_of(at * width, 128), width)

    def copy_of(h, src, dst, sem, to):
        return pltpu.make_async_remote_copy(
            src_ref=src, dst_ref=dst, send_sem=sends.at[h, sem], recv_sem=recvs.at[h, sem],
            device_id=to, device_id_type=pl.DeviceIdType.MESH,
        )

    def first(h, k):
        return copy_of(
            h, part.at[h, :, block(turn(g, k))], inbox.at[h, k - 1], k - 1, (p, turn(g, k), c)
        )

    def along(h, k):
        return copy_of(h, blocks.at[h, g], blocks.at[h, g], n + k - 1, (p, turn(g, k), c))

    def flat(h, k):
        return copy_of(h, cols.at[me, h], cols.at[me, h], 2 * n + k - 1, (turn(p, k), g, c))

    def across(h, k):
        return copy_of(
            h, blocks.at[h, turn(p, k)], rows.at[me, h], 3 * n + k - 1, (turn(p, k), g, c)
        )

    def over(h, k, ref, base):
        slot = turn(p, count - k) * 2 + c
        return copy_of(h, ref.at[slot, h], ref.at[slot, h], base + k, (p, g, 1 - c))

    def pass_on(h, b):
        @pl.when(b != p)
        def _():
            copy_of(
                h, blocks.at[h, b], rows.at[me, h], 3 * n + turn(b, count - p) - 1, (b, g, c)
            ).start()

        @pl.when(b == p)
        def _():
            rows[me, h] = blocks[h, p]
            over(h, 0, rows, 5 * n + 1).start()

    def stage_sum(h):
        total = part[h, :, block(g)].astype(f32)
        for k in range(1, count):
            first(h, k).wait_recv()
            total += inbox[h, k - 1].astype(f32)
        mine = total.astype(bf16)
        blocks[h, g] = mine
        cols[me, h] = mine
        for k in range(1, count):
            along(h, k).start()
        for k in range(1, count):
            flat(h, k).start()
        over(h, 0, cols, 4 * n).start()
        pass_on(h, g)

    def stage_across(h):
        for k in range(1, count):
            flat(h, k).wait_recv()
            over(h, k, cols, 4 * n).start()
            along(h, k).wait_recv()
            pass_on(h, turn(g, count - k))

    def stage_rows(h):
        for k in range(1, count):
            across(h, k).wait_recv()
            over(h, k, rows, 5 * n + 1).start()

    @pl.when((band == 0) & (step == 0))
    def _():
        index[...] = row_index(gvec[0:1, :], gvec[1:2, :], gvec[2:3, :])
        pltpu.make_async_copy(index, idx, outs.at[0]).start()
        barrier = pltpu.get_barrier_semaphore()
        for k in range(1, count):
            pl.semaphore_signal(barrier, inc=1, device_id=(p, turn(g, k), c))
            pl.semaphore_signal(barrier, inc=1, device_id=(turn(p, k), g, c))
        pl.semaphore_signal(barrier, inc=1, device_id=(p, g, 1 - c))

    @pl.when(band == 0)
    def _():
        for y in range(STEP // N):
            yy = step * (STEP // N) + y
            l1 = left[0, pl.ds(yy, 1), :]
            l2 = left[1, pl.ds(yy, 1), :]
            tabs[step, y * N : (y + 1) * N, :] = (l1 * right[0] + l2 * right[1]).astype(bf16)

    @pl.when(step == 0)
    def _():
        acc_ee[...] = jnp.zeros_like(acc_ee)
        acc_eo[...] = jnp.zeros_like(acc_eo)
        acc_o[...] = jnp.zeros_like(acc_o)

    def products(v, carry):
        d0, d1, d2, d3 = [
            (a[pl.ds(2 * v, 2)].astype(f32) * b[band].astype(f32)[None]).reshape(2 * planes, STEP)
            for a, b in ((v0, c0), (v1, c1), (v2, c2), (v3, c3))
        ]
        e0, e1 = d0 + d2, d1 + d3
        at = pl.multiple_of(v * 2 * planes, 16)
        where = pl.ds(at, 2 * planes)
        ee[where, :] = (e0 + e1).astype(bf16)
        eo[where, :] = (e0 - e1).astype(bf16)
        oo[where, :] = (d0 - d2).astype(bf16)
        oo[pl.ds(pl.multiple_of(height + at, 16), 2 * planes), :] = (d1 - d3).astype(bf16)
        return carry

    lax.fori_loop(0, nv // 2, products, 0)
    acc_ee[...] += jnp.dot(ee[...], tabs[step, :, 0:256], preferred_element_type=f32)
    acc_eo[...] += jnp.dot(eo[...], tabs[step, :, 256:512], preferred_element_type=f32)

    def multiply(i, carry):
        at = pl.ds(pl.multiple_of(i * height, 16), height)
        acc_o[at, :] += jnp.dot(oo[at, :], tabs[step, :, 512:1024], preferred_element_type=f32)
        return carry

    lax.fori_loop(0, 2, multiply, 0)

    @pl.when((band == 0) & (step == steps - 1))
    def _():
        pltpu.make_async_copy(index, idx, outs.at[0]).wait()
        pl.semaphore_wait(pltpu.get_barrier_semaphore(), 2 * count - 1)

    for h in range(1, bands):
        @pl.when((band == h) & (step == steps - 2))
        def _():
            stage_sum(h - 1)

        @pl.when((band == h) & (step == steps - 1))
        def _():
            stage_across(h - 1)

    @pl.when((band == 0) & (step == 0))
    def _():
        own = lax.broadcasted_iota(jnp.int32, (1, RAD * 4 * nv), 1) % nv

        weights = [xtab[h, pl.ds(pl.multiple_of(g * planes, 8), planes), :] for h in range(2)]

        def place(v, carry):
            for h in range(2):
                two = [jnp.where(own == 2 * v + u, weights[h], 0.0) for u in range(2)]
                at = pl.multiple_of(h * height + v * 2 * planes, 16)
                xmat[pl.ds(at, 2 * planes), :] = jnp.concatenate(two, 0).astype(bf16)
            return carry

        lax.fori_loop(0, nv // 2, place, 0)

    @pl.when(step == steps - 1)
    def _():
        lane = lax.broadcasted_iota(jnp.int32, (1, lanes), 1) % nv
        occupied = jnp.zeros((1, lanes), jnp.int32)
        energy = jnp.zeros((1, lanes), f32)
        for v in range(nv):
            occupied = jnp.where(lane == v, occ[v], occupied)
            energy = jnp.where(lane == v, val_e[v], energy)
        gap = cond_e[me * bands + band] - energy
        factor = jnp.sqrt(occupied.astype(f32) / (4.0 * gap)) * (1.0 / N**1.5)
        w = WIDTHS[2]
        top, low = acc_o[0:height, :], acc_o[height : 2 * height, :]
        odd_p = top[:, 0:w] - sign[...] * low[:, w:]
        odd_q = top[:, w:] + sign[...] * low[:, 0:w]
        groups = (
            (acc_ee[:, 0:128], acc_ee[:, 128:256]),
            (acc_eo[:, 0:128], acc_eo[:, 128:256]),
            (odd_p, odd_q),
        )
        for (p_part, q_part), size, start in zip(groups, ROWS, STARTS):
            p_rows = p_part.T[0:size].astype(bf16)
            q_rows = q_part.T[0:size].astype(bf16)
            summed = jnp.dot(p_rows, xmat[0:height, :], preferred_element_type=f32)
            summed += jnp.dot(q_rows, xmat[height : 2 * height, :], preferred_element_type=f32)
            for t in range(RAD // per_tile):
                piece = summed[:, t * lanes : (t + 1) * lanes] * factor
                for u in range(2 * per_tile):
                    a = t * per_tile + u // 2
                    at = ((u % 2) * RAD + a) * NR + start
                    turned = pltpu.roll(piece, lanes - 2 * nv * u, 1) if u else piece
                    sec[at : at + size, :] = turned

        def pick(i, carry):
            for u in range(16):
                got[pl.ds(i * 16 + u, 1), :] = sec[pl.ds(idx[0, i * 16 + u], 1), :]
            return carry

        halves = KG // width
        for q in range(halves):
            lax.fori_loop(q * width // 16, (q + 1) * width // 16, pick, 0)
            for i in range(q * width // 384, (q + 1) * width // 384):
                turned = got[i * 384 : (i + 1) * 384, :].T.astype(bf16)
                part[band, :, i * 384 : (i + 1) * 384] = turned[0:nv]
                part[band, :, KG + i * 384 : KG + (i + 1) * 384] = turned[nv : 2 * nv]
            for k in range(1, count):
                @pl.when(lax.rem(turn(g, k), halves) == q)
                def _():
                    first(band, k).start()

    for h in range(bands):
        @pl.when((band == h) & (step == steps - 1))
        def _():
            if h:
                stage_rows(h - 1)
            if h == bands - 1:
                stage_sum(h)
                stage_across(h)
                stage_rows(h)
                for q in range(bands):
                    for k in range(count):
                        over(q, k, cols, 4 * n).wait_recv()
                first_out = pltpu.make_async_copy(cols, cols_out, outs.at[0])
                first_out.start()
                for q in range(bands):
                    for k in range(count):
                        over(q, k, rows, 5 * n + 1).wait_recv()
                second_out = pltpu.make_async_copy(rows, rows_out, outs.at[1])
                second_out.start()
                for q in range(bands):
                    for k in range(1, count):
                        first(q, k).wait_send()
                        along(q, k).wait_send()
                        flat(q, k).wait_send()
                        across(q, k).wait_send()
                    for k in range(count):
                        over(q, k, cols, 4 * n).wait_send()
                        over(q, k, rows, 5 * n + 1).wait_send()
                first_out.wait()
                second_out.wait()


def product_kernel(prefactor, rows, cols, out, turned):
    share, tile = out.shape
    c = lax.axis_index("gcol")
    low = share // 128 * 128
    shift = share - low

    @pl.when(pl.program_id(0) == 0)
    def _():
        span = turned.shape[0]
        turned[...] = rows[:, pl.ds(pl.multiple_of(c * low, 128), span)].T

    left = turned[pl.ds(pl.multiple_of(c * shift, 16), share), :]
    out[...] = jnp.dot(left, cols[...], preferred_element_type=jnp.float32) * prefactor


def product(rows, cols, share, prefactor):
    depth, width = rows.shape
    low = share // 128 * 128
    tile = 384
    return pl.pallas_call(
        functools.partial(product_kernel, prefactor),
        out_shape=jax.ShapeDtypeStruct((share, width), jnp.float32),
        grid=(width // tile,),
        in_specs=[
            pl.BlockSpec((depth, width), lambda i: (0, 0)),
            pl.BlockSpec((depth, tile), lambda i: (0, i)),
        ],
        out_specs=pl.BlockSpec((share, tile), lambda i: (0, i)),
        scratch_shapes=[pltpu.VMEM((width - low, depth), jnp.bfloat16)],
    )(rows, cols)


def fast_body(valence, conduction, val_energy, cond_energy, val_occupation, gvectors):
    nv, planes, _ = valence.shape
    bands = conduction.shape[0]
    count = lax.axis_size("pair")
    gcol_count = lax.axis_size("gcol")
    height = nv * planes
    steps = QUARTER // STEP
    width = 2 * KG // count
    slots = count * gcol_count
    bf16, f32 = jnp.bfloat16, jnp.float32
    left, right, sign = half_plane_tables()
    whole = lambda shape: pl.BlockSpec(shape, lambda b, i: (0,) * len(shape))
    piece = lambda size, q: pl.BlockSpec(
        (size, planes, STEP), lambda b, i, q=q: (0, 0, q * steps + i)
    )
    smem = pl.BlockSpec(memory_space=pltpu.SMEM)
    gathered = jax.ShapeDtypeStruct((slots, bands, nv, width), bf16)
    sems = 6 * (count - 1) + 2
    cols, rows = pl.pallas_call(
        chi_kernel,
        out_shape=(gathered, gathered),
        grid_spec=pltpu.PrefetchScalarGridSpec(
            num_scalar_prefetch=0,
            grid=(bands, steps),
            in_specs=[smem] * 3
            + [whole((3, KG))]
            + [piece(nv, q) for q in range(4)]
            + [piece(bands, q) for q in range(4)]
            + [
                whole(left.shape),
                whole(right.shape),
                whole(sign.shape),
                whole((2, N, RAD * 4 * nv)),
            ],
            out_specs=(pl.BlockSpec(memory_space=pl.ANY), pl.BlockSpec(memory_space=pl.ANY)),
            scratch_shapes=[
                pltpu.VMEM((height, STEP), bf16),
                pltpu.VMEM((height, STEP), bf16),
                pltpu.VMEM((2 * height, STEP), bf16),
                pltpu.VMEM((steps, STEP, 2 * sum(WIDTHS)), bf16),
                pltpu.VMEM((height, 2 * WIDTHS[0]), f32),
                pltpu.VMEM((height, 2 * WIDTHS[1]), f32),
                pltpu.VMEM((2 * height, 2 * WIDTHS[2]), f32),
                pltpu.VMEM((2 * height, RAD * 4 * nv), bf16),
                pltpu.VMEM((2 * RAD * NR, 128), f32),
                pltpu.VMEM((KG, 128), f32),
                pltpu.VMEM((bands, nv, 2 * KG), bf16),
                pltpu.VMEM((bands, count - 1, nv, width), bf16),
                pltpu.VMEM((bands, count, nv, width), bf16),
                pltpu.VMEM((slots, bands, nv, width), bf16),
                pltpu.VMEM((slots, bands, nv, width), bf16),
                pltpu.VMEM((1, KG), jnp.int32),
                pltpu.SMEM((1, KG), jnp.int32),
                pltpu.SemaphoreType.DMA((bands, sems)),
                pltpu.SemaphoreType.DMA((bands, sems)),
                pltpu.SemaphoreType.DMA((2,)),
            ],
        ),
        compiler_params=pltpu.CompilerParams(
            vmem_limit_bytes=60 * 1024 * 1024, collective_id=0, has_side_effects=True
        ),
    )(
        val_occupation, val_energy, cond_energy, gvectors,
        *([valence] * 4), *([conduction] * 4), left, right, sign, plane_table(nv),
    )
    all_pairs = slots * bands * nv
    prefactor = -1.0 / math.sqrt(all_pairs)
    cols = cols.reshape(all_pairs, width)
    rows = rows.reshape(all_pairs, width)
    share = width // gcol_count
    return product(rows, cols, share, prefactor)


def solution(mesh):
    sizes = dict(mesh.shape)
    fast = sizes["pair"] == sizes["grow"] and sizes["gcol"] == 2 and N // sizes["grow"] % 8 == 0
    return jax.shard_map(
        fast_body if fast else body,
        mesh=mesh,
        in_specs=(P(None, "grow", None), P(("pair", "gcol"), "grow", None), P(), P(), P(), P()),
        out_specs=P(("pair", "gcol"), "grow"),
        check_vma=False,
    )
```

profile of v0, /device:TPU:27, one launch (start us, length us, event | category | flops | bytes accessed | tf_op | source)
XLA Modules:
  0.0 58.7 jit_solution(14785838684674821772)
XLA Ops:
  0.0 52.5 %shard_map.100 = (bf16[8,2,16,1920]{3,2,1,0:T(8,128)(2,1)}, bf16[8,2,16,1920]{3,2,1,0:T(8,128)(2,1)}) custom-call(s32[16]{0:T(128)} %occ.1, f32[16]{0:T(128)} %val_e.1, f32[16]{0:T(128)} %cond_e.1, s32[3,3840]{1,0:T(4,128)} %gvec.1, bf16[16,24,9216]{2,1,0:T(8,128)(2,1)} %v3.1, bf16[16,24,9216]{2,1,0:T(8,128)(2,1)} %v3.1, bf16[16,24,9216]{2,1,0:T(8,128)(2,1)} %v3.1, ...), custom_call_target="tpu_custom_call" | custom-call | tf_op jit(solution)/shard_map/pallas_call | solution.py:442
  52.5 6.3 %shard_map.101 = f32[960,1920]{1,0:T(8,128)} custom-call(bf16[256,1920]{1,0:T(8,128)(2,1)} %bitcast.3, bf16[256,1920]{1,0:T(8,128)(2,1)} %bitcast.2), custom_call_target="tpu_custom_call" | custom-call | tf_op jit(solution)/shard_map/pallas_call | solution.py:411
where the time goes:
time: 59.4 us; the launch traced here: 58.7 us
  Pallas kernels  58.7 us (99%)
    pallas_call x1, Pallas kernels, fast_body(): pl.pallas_call(chi_kernel, out_shape=(gathered, gathered), grid_spec=pltp...  52.5 us
    pallas_call x1, Pallas kernels, product(): pl.pallas_call(functools.partial(product_kernel, prefactor), out_shape=ja...  6.26 us

commit v1 on v0

v1 whole, which is shorter than its diff:
```python
import functools
import math

import jax
import jax.numpy as jnp
import numpy as np
from jax import lax
from jax.experimental import pallas as pl
from jax.experimental.pallas import tpu as pltpu
from jax.sharding import PartitionSpec as P

N = 96
RAD = 12
KG = 3840
NV = 16


def wave_tables(positions, frequencies):
    phases = jnp.mod(positions[:, None] * frequencies[None, :], N).astype(jnp.float32) * (
        2.0 * math.pi / N
    )
    return (jnp.cos(phases), jnp.sin(phases))


def build_tables(x_positions):
    all_freq = jnp.arange(-RAD, RAD + 1, dtype=jnp.int32)
    pos_freq = jnp.arange(1, RAD + 1, dtype=jnp.int32)
    positions = jnp.arange(N, dtype=jnp.int32)
    cosine, sine_part = wave_tables(positions, all_freq)
    z_table = jnp.concatenate([cosine, sine_part], 1).astype(jnp.bfloat16)
    y_table = jnp.stack(
        [jnp.stack([cosine, sine_part], 1), jnp.stack([-sine_part, cosine], 1)], 1
    ).astype(jnp.bfloat16)
    x_cos, x_sin = wave_tables(x_positions, pos_freq)
    x_table = jnp.stack([jnp.stack([x_cos, -x_sin], 1), jnp.stack([-x_sin, -x_cos], 1)], 1).astype(
        jnp.bfloat16
    )
    return (z_table, y_table, x_table)


def pair_product(left_rows, right_rows):
    return lax.dot_general(
        left_rows, right_rows, (((0,), (0,)), ((), ())), preferred_element_type=jnp.float32
    )


def body(valence, conduction, val_energy, cond_energy, val_occupation, gvectors):
    pair_count = lax.axis_size("pair")
    gcol_count = lax.axis_size("gcol")
    planes = valence.shape[1]
    cond_bands = conduction.shape[0]
    extent = 2 * RAD + 1
    local_pairs = cond_bands * NV
    x_positions = lax.axis_index("grow") * planes + jnp.arange(planes, dtype=jnp.int32)
    z_table, y_table, x_table = build_tables(x_positions)
    flat_index = ((gvectors[0] - 1) * extent + gvectors[1] + RAD) * extent + gvectors[2] + RAD
    density = conduction[:, None] * valence[None]
    section_one = jnp.dot(
        density.reshape(-1, N), z_table, preferred_element_type=jnp.float32
    ).astype(jnp.bfloat16)
    section_one = section_one.reshape(local_pairs * planes, N, 2, extent)
    second = jnp.einsum(
        "ayik,yioj->aojk", section_one, y_table, preferred_element_type=jnp.float32
    ).astype(jnp.bfloat16)
    second = second.reshape(local_pairs, planes, 2, extent * extent)
    section_three = jnp.einsum(
        "pxoq,xosm->psmq", second, x_table, preferred_element_type=jnp.float32
    )
    section_three = section_three.reshape(local_pairs, 2, RAD * extent * extent)
    picked = jnp.take(section_three, flat_index, axis=2).reshape(local_pairs, 2 * KG)
    summed = lax.psum_scatter(
        picked.astype(jnp.bfloat16), "grow", scatter_dimension=1, tiled=True
    ).astype(jnp.float32)
    first_band = (lax.axis_index("pair") * gcol_count + lax.axis_index("gcol")) * cond_bands
    own_energy = lax.dynamic_slice_in_dim(cond_energy, first_band, cond_bands, 0)
    weight = val_occupation.astype(jnp.float32)[None, :] / (
        4.0 * (own_energy[:, None] - val_energy[None, :])
    )
    factor = (jnp.sqrt(weight) * (1.0 / N**1.5)).reshape(local_pairs, 1)
    weighted = (summed * factor).astype(jnp.bfloat16)
    prefactor = -1.0 / math.sqrt(pair_count * gcol_count * local_pairs)
    full_rows = lax.all_gather(weighted, "grow", axis=1, tiled=True)
    row_part = lax.all_to_all(full_rows, "pair", split_axis=1, concat_axis=0, tiled=True)
    partial_value = pair_product(row_part, lax.all_gather(weighted, "pair", axis=0, tiled=True))
    return lax.psum_scatter(
        (partial_value * prefactor).astype(jnp.bfloat16), "gcol", scatter_dimension=0, tiled=True
    ).astype(jnp.float32)


EXT = 2 * RAD + 1
QUARTER = N * N // 4
STEP = 8 * N
CLASSES = ((0, 4, 8, 12), (2, 6, 10), (1, 3, 5, 7, 9, 11))
WIDTHS = (128, 128, 256)
ROWS = (104, 80, 152)
STARTS = (0, 104, 184)
NR = 336
TALL = (112, 80, 160)
PIECE = 384
LAG = 3


def half_plane_tables():
    total = 2 * sum(WIDTHS)
    left = np.zeros((2, N // 4, total), np.float32)
    right = np.zeros((2, N, total), np.float32)
    sign = np.zeros((1, WIDTHS[2]), np.float32)
    y = np.arange(N // 4)[:, None]
    z = np.arange(N)[:, None]
    k = np.arange(-RAD, RAD + 1)
    base = 0
    for freqs, width in zip(CLASSES, WIDTHS):
        jj = np.repeat(np.array(freqs), EXT)[None]
        kk = np.tile(k, len(freqs))[None]
        count = jj.shape[1]
        ay = 2 * np.pi * ((jj * y) % N) / N
        az = 2 * np.pi * ((kk * z) % N) / N
        for part in range(2):
            cols = slice(base + part * width, base + part * width + count)
            left[0, :, cols] = np.sin(ay) if part else np.cos(ay)
            left[1, :, cols] = np.cos(ay) if part else -np.sin(ay)
            right[0, :, cols] = np.cos(az)
            right[1, :, cols] = np.sin(az)
        base += 2 * width
    jj = np.repeat(np.array(CLASSES[2]), EXT)
    sign[0, : jj.size] = np.where(jj % 4 == 1, 1.0, -1.0)
    return left, right, sign


def plane_table(pairs):
    x = np.arange(N)[:, None]
    a = np.arange(1, RAD + 1)[None]
    ang = 2 * np.pi * ((a * x) % N) / N
    c, s = np.cos(ang), np.sin(ang)
    tab = np.stack([np.stack([c, -s, c, -s], -1), np.stack([-s, -c, s, c], -1)])
    return np.repeat(tab.reshape(2, N, RAD * 4), pairs, axis=2).astype(np.float32)


def row_index(a, b, d):
    j = jnp.abs(b)
    k = jnp.where(b < 0, -d, d) + RAD
    row = jnp.where(
        (j & 1) == 1,
        STARTS[2] + (j >> 1) * EXT,
        jnp.where((j & 3) == 2, STARTS[1], STARTS[0]) + (j >> 2) * EXT,
    )
    return jnp.maximum((a - 1) * NR + row + k, 0)


def chi_kernel(
    occ, val_e, cond_e, gvec, val, cond, left, right, sign, xtab,
    cols_out, rows_out,
    vbuf, cbuf, leftv, rightv, signv, xv, tabs_e, tabs_o,
    ee0, eo0, od0, ee1, eo1, od1, acc_e, acc_o, xmat, sec, got,
    part, rin, lin, rout, lout, tot, cols, rows, index, idx,
    loads, chain_send, chain_recv, row_send, row_recv, col_send, col_recv,
    over_send, over_recv, outs,
):
    f32, bf16 = jnp.float32, jnp.bfloat16
    nv, planes, _ = val.shape
    bands = cond.shape[0]
    height = nv * planes
    pairs = bands * nv
    lanes = 128
    half = lanes // 2
    steps = QUARTER // STEP
    pieces = part.shape[0]
    slots, _, width = cols.shape
    count = slots // 2
    per = width // PIECE
    middle = per // 2
    span = rows.shape[2]
    low = width - span
    p, g, c = lax.axis_index("pair"), lax.axis_index("grow"), lax.axis_index("gcol")
    me = p * 2 + c
    turn = lambda at, k: lax.rem(at + k, count)

    def remote(src, dst, send, recv, to):
        return pltpu.make_async_remote_copy(
            src_ref=src, dst_ref=dst, send_sem=send, recv_sem=recv,
            device_id=to, device_id_type=pl.DeviceIdType.MESH,
        )

    table_loads = [
        pltpu.make_async_copy(a, b, loads.at[8 * steps + i])
        for i, (a, b) in enumerate(
            (
                (left, leftv),
                (right, rightv),
                (sign, signv),
                (xtab.at[:, pl.ds(pl.multiple_of(g * planes, 8), planes), :], xv),
            )
        )
    ]
    step_loads = []
    for s in range(steps):
        group = []
        for q in range(4):
            at = pl.ds(q * QUARTER + s * STEP, STEP)
            for u, (a, b) in enumerate(((cond, cbuf), (val, vbuf))):
                group.append(
                    pltpu.make_async_copy(
                        a.at[:, :, at], b.at[:, :, at], loads.at[8 * s + 2 * q + u]
                    )
                )
        step_loads.append(group)
    for copy in table_loads[:3]:
        copy.start()
    for copy in step_loads[0]:
        copy.start()
    table_loads[3].start()
    for group in step_loads[1:]:
        for copy in group:
            copy.start()

    barrier = pltpu.get_barrier_semaphore()
    pl.semaphore_signal(barrier, inc=1, device_id=(p, g, 1 - c))
    for k in range(1, count):
        for d in range(2):
            pl.semaphore_signal(barrier, inc=1, device_id=(turn(p, k), g, d))
        pl.semaphore_signal(barrier, inc=1, device_id=(p, turn(g, k), c))

    index[...] = row_index(gvec[0:1, :], gvec[1:2, :], gvec[2:3, :])
    index_copy = pltpu.make_async_copy(index, idx, outs.at[0])
    index_copy.start()

    for copy in table_loads[:3]:
        copy.wait()

    def table_rows(y, carry):
        l1 = leftv[0, pl.ds(y, 1), :]
        l2 = leftv[1, pl.ds(y, 1), :]
        full = l1 * rightv[0] + l2 * rightv[1]
        w = WIDTHS[2]
        odd_p, odd_q = full[:, 512 : 512 + w], full[:, 512 + w :]
        tabs_e[pl.ds(pl.multiple_of(y * N, 32), N), :] = full[:, 0:512].astype(bf16)
        s = y // (STEP // N)
        at = pl.multiple_of((y - s * (STEP // N)) * N, 32)
        tabs_o[s, pl.ds(at, N), 0:w] = odd_p.astype(bf16)
        tabs_o[s, pl.ds(at, N), w:] = odd_q.astype(bf16)
        tabs_o[s, pl.ds(STEP + at, N), 0:w] = (odd_q * (0.0 - signv[...])).astype(bf16)
        tabs_o[s, pl.ds(STEP + at, N), w:] = (odd_p * signv[...]).astype(bf16)
        return carry

    lax.fori_loop(0, QUARTER // N, table_rows, 0)

    def products(s, ee, eo, od):
        for copy in step_loads[s]:
            copy.wait()
        for b in range(bands):
            for m in range(STEP // lanes):
                at = [pl.ds(q * QUARTER + s * STEP + m * lanes, lanes) for q in range(4)]
                here = slice(m * lanes, (m + 1) * lanes)
                there = slice(STEP + m * lanes, STEP + (m + 1) * lanes)
                cs = [cbuf[b, :, q].astype(f32)[None] for q in at]
                for v in range(0, nv, 2):
                    d0, d1, d2, d3 = [
                        (vbuf[v : v + 2, :, q].astype(f32) * u).reshape(2 * planes, lanes)
                        for q, u in zip(at, cs)
                    ]
                    e0, e1 = d0 + d2, d1 + d3
                    row = b * height + v * planes
                    where = slice(row, row + 2 * planes)
                    ee[where, here] = (e0 + e1).astype(bf16)
                    eo[where, here] = (e0 - e1).astype(bf16)
                    od[where, here] = (d0 - d2).astype(bf16)
                    od[where, there] = (d1 - d3).astype(bf16)

    def multiply(s, ee, eo, od):
        at = slice(s * STEP, (s + 1) * STEP)
        parts = (
            (acc_e, slice(0, 256), jnp.dot(ee[...], tabs_e[at, 0:256], preferred_element_type=f32)),
            (acc_e, slice(256, 512), jnp.dot(eo[...], tabs_e[at, 256:512], preferred_element_type=f32)),
            (acc_o, slice(0, 512), jnp.dot(od[...], tabs_o[s], preferred_element_type=f32)),
        )
        for acc, where, value in parts:
            if s:
                acc[:, where] += value
            else:
                acc[:, where] = value

    sets = ((ee0, eo0, od0), (ee1, eo1, od1))
    products(0, *sets[0])
    for s in range(steps):
        if s + 1 < steps:
            products(s + 1, *sets[(s + 1) % 2])
        multiply(s, *sets[s % 2])

    table_loads[3].wait()
    own = lax.broadcasted_iota(jnp.int32, (1, RAD * 4 * nv), 1) % nv

    def place(v, carry):
        for h in range(2):
            two = [jnp.where(own == 2 * v + u, xv[h], 0.0) for u in range(2)]
            at = pl.multiple_of(h * height + v * 2 * planes, 16)
            xmat[pl.ds(at, 2 * planes), :] = jnp.concatenate(two, 0).astype(bf16)
        return carry

    lax.fori_loop(0, nv // 2, place, 0)

    lane = lax.broadcasted_iota(jnp.int32, (1, lanes), 1)
    occupied = jnp.zeros((1, lanes), jnp.int32)
    energy = jnp.zeros((1, lanes), f32)
    for v in range(nv):
        occupied = jnp.where(lane % nv == v, occ[v], occupied)
        energy = jnp.where(lane % nv == v, val_e[v], energy)
    factors = [
        jnp.sqrt(occupied.astype(f32) / (4.0 * (cond_e[me * bands + b] - energy)))
        * (1.0 / N**1.5)
        for b in range(bands)
    ]
    lower = lane < half
    groups = (
        (acc_e, 0, 128, TALL[0], ROWS[0], STARTS[0]),
        (acc_e, 256, 128, TALL[1], ROWS[1], STARTS[1]),
        (acc_o, 0, 256, TALL[2], ROWS[2], STARTS[2]),
    )
    for acc, base, w, tall, size, start in groups:
        summed = []
        for b in range(bands):
            at = slice(b * height, (b + 1) * height)
            turned = [
                acc[at, base + h * w : base + (h + 1) * w].astype(bf16).T[0:tall] for h in range(2)
            ]
            summed.append(
                jnp.dot(jnp.concatenate(turned, 1), xmat[...], preferred_element_type=f32)
            )
        for t in range(RAD // 2):
            first, second = [
                summed[b][0:size, t * lanes : (t + 1) * lanes] * factors[b] for b in range(bands)
            ]
            second = pltpu.roll(second, half, 1)
            at = 2 * t * NR + start
            sec[at : at + size, :] = jnp.where(lower, first, second)
            sec[at + NR : at + NR + size, :] = jnp.where(lower, second, first)

    index_copy.wait()
    pl.semaphore_wait(barrier, 1 + 3 * (count - 1))

    def pick(n):
        for u in range(PIECE):
            got[u : u + 1, :] = sec[pl.ds(idx[0, n * PIECE + u], 1), :]
        turned = got[...].T
        at = slice(n * PIECE, (n + 1) * PIECE)
        odd = ((gvec[0:1, at] - 1) & 1) == 1
        flip = gvec[1:2, at] < 0
        top, bottom = turned[0:half], turned[half:lanes]
        for b, both in enumerate((jnp.where(odd, bottom, top), jnp.where(odd, top, bottom))):
            chosen = jnp.where(flip, both[2 * nv : 4 * nv], both[0 : 2 * nv]).astype(bf16)
            part[n, b * nv : (b + 1) * nv, :] = chosen[0:nv]
            part[n, pairs + b * nv : pairs + (b + 1) * nv, :] = chosen[nv : 2 * nv]

    def right_copy(src, t):
        return remote(
            src.at[t], rin.at[t], chain_send.at[0, t], chain_recv.at[0, t],
            (p, jnp.minimum(g + 1, count - 1), c),
        )

    def left_copy(src, t):
        return remote(
            src.at[t], lin.at[t], chain_send.at[1, t], chain_recv.at[1, t],
            (p, jnp.maximum(g - 1, 0), c),
        )

    def chain(t, make, came, passed, first, last):
        @pl.when((t >= 0) & (t < pieces))
        def _():
            @pl.when(first)
            def _():
                make(part, t).start()

            @pl.when(jnp.logical_not(first))
            def _():
                make(part, t).wait_recv()

                @pl.when(jnp.logical_not(last))
                def _():
                    passed[t] = (part[t].astype(f32) + came[t].astype(f32)).astype(bf16)
                    make(passed, t).start()

    def row_copy(t, r, b, d, lo, wide, to):
        return remote(
            tot.at[t, pl.ds(r * pairs, pairs), pl.ds(lo, wide)],
            rows.at[me, :, pl.ds(to, wide)],
            row_send.at[t, r, d], row_recv.at[me], (b, g, d),
        )

    def put(t, r, b, d, lo, wide, to):
        here = (b == p) & (d == c)

        @pl.when(here)
        def _():
            rows[me, :, pl.ds(to, wide)] = tot[t, r * pairs : (r + 1) * pairs, lo : lo + wide]

        @pl.when(jnp.logical_not(here))
        def _():
            row_copy(t, r, b, d, lo, wide, to).start()

    def col_copy(t, r, j, k):
        at = pl.ds(pl.multiple_of(j * PIECE, 128), PIECE)
        return remote(
            tot.at[t, pl.ds(r * pairs, pairs), :], cols.at[me, :, at],
            col_send.at[j, k - 1], col_recv.at[p], (turn(p, k), g, c),
        )

    def finish(t):
        @pl.when((t >= 0) & (t < pieces))
        def _():
            mine = lambda: part[t].astype(f32)

            @pl.when(g == 0)
            def _():
                tot[t] = (mine() + lin[t].astype(f32)).astype(bf16)

            @pl.when(g == count - 1)
            def _():
                tot[t] = (mine() + rin[t].astype(f32)).astype(bf16)

            @pl.when((g > 0) & (g < count - 1))
            def _():
                tot[t] = (mine() + rin[t].astype(f32) + lin[t].astype(f32)).astype(bf16)

            h = t // per
            j = t - h * per
            for r in range(2):
                b = h + r * (count // 2)

                @pl.when(j < middle)
                def _():
                    put(t, r, b, 0, 0, PIECE, pl.multiple_of(j * PIECE, 128))

                @pl.when(j > middle)
                def _():
                    put(t, r, b, 1, 0, PIECE, pl.multiple_of(j * PIECE - low, 128))

                @pl.when(j == middle)
                def _():
                    put(t, r, b, 0, 0, span - middle * PIECE, middle * PIECE)
                    put(t, r, b, 1, low - middle * PIECE, (middle + 1) * PIECE - low, 0)

                @pl.when(b == g)
                def _():
                    at = pl.ds(pl.multiple_of(j * PIECE, 128), PIECE)
                    cols[me, :, at] = tot[t, r * pairs : (r + 1) * pairs, :]
                    for k in range(1, count):
                        col_copy(t, r, j, k).start()

    for n in range(pieces + LAG * (count - 1)):
        if n < pieces:
            pick(n)
        to_right = n - g * LAG
        to_left = n - (count - 1 - g) * LAG
        chain(to_right, right_copy, rin, rout, g == 0, g == count - 1)
        chain(to_left, left_copy, lin, lout, g == count - 1, g == 0)
        finish(jnp.minimum(to_right, to_left))

    def over(q, core):
        slot = q * 2 + core
        return remote(
            cols.at[slot], cols.at[slot], over_send.at[q], over_recv.at[q], (p, g, 1 - c)
        )

    def out_copy(ref, dst, slot, which):
        return pltpu.make_async_copy(ref.at[slot], dst.at[slot], outs.at[1 + which * slots + slot])

    over(p, c).start()
    out_copy(cols, cols_out, me, 0).start()
    for k in range(1, count):
        q = turn(p, k)
        at = q * 2 + c
        remote(cols.at[at], cols.at[at], col_send.at[0, 0], col_recv.at[q], (q, g, c)).wait_recv()
        over(q, c).start()
        out_copy(cols, cols_out, at, 0).start()
    for slot in range(slots):
        @pl.when(slot != me)
        def _():
            remote(
                rows.at[slot], rows.at[slot], row_send.at[0, 0, 0], row_recv.at[slot],
                (slot // 2, g, slot % 2),
            ).wait_recv()

        out_copy(rows, rows_out, slot, 1).start()
    for k in range(count):
        q = turn(p, k)
        over(q, 1 - c).wait_recv()
        out_copy(cols, cols_out, q * 2 + 1 - c, 0).start()

    for t in range(pieces):
        @pl.when(g < count - 1)
        def _():
            right_copy(part, t).wait_send()

        @pl.when(g > 0)
        def _():
            left_copy(part, t).wait_send()

        h, j = t // per, t % per
        for r in range(2):
            b = h + r * (count // 2)
            for d in range(2):
                if (j < middle and d == 1) or (j > middle and d == 0):
                    continue
                wide = PIECE
                if j == middle:
                    wide = (middle + 1) * PIECE - low if d else span - middle * PIECE

                @pl.when(jnp.logical_not((p == b) & (c == d)))
                def _():
                    row_copy(t, r, b, d, 0, wide, 0).wait_send()

            @pl.when(g == b)
            def _():
                for k in range(1, count):
                    col_copy(t, r, j, k).wait_send()

    for q in range(count):
        over(q, c).wait_send()
    for slot in range(slots):
        out_copy(cols, cols_out, slot, 0).wait()
        out_copy(rows, rows_out, slot, 1).wait()


def product_kernel(prefactor, rows, cols, out, turned):
    share = out.shape[0]
    c = lax.axis_index("gcol")
    shift = rows.shape[1] - share

    @pl.when(pl.program_id(0) == 0)
    def _():
        turned[...] = rows[...].T

    left = turned[pl.ds(pl.multiple_of(c * shift, 16), share), :]
    out[...] = jnp.dot(left, cols[...], preferred_element_type=jnp.float32) * prefactor


def product(rows, cols, share, prefactor):
    depth, width = cols.shape
    span = rows.shape[1]
    tile = 384
    return pl.pallas_call(
        functools.partial(product_kernel, prefactor),
        out_shape=jax.ShapeDtypeStruct((share, width), jnp.float32),
        grid=(width // tile,),
        in_specs=[
            pl.BlockSpec((depth, span), lambda i: (0, 0)),
            pl.BlockSpec((depth, tile), lambda i: (0, i)),
        ],
        out_specs=pl.BlockSpec((share, tile), lambda i: (0, i)),
        scratch_shapes=[pltpu.VMEM((span, depth), jnp.bfloat16)],
    )(rows, cols)


def fast_body(valence, conduction, val_energy, cond_energy, val_occupation, gvectors):
    nv, planes, points = valence.shape
    bands = conduction.shape[0]
    count = lax.axis_size("pair")
    gcol_count = lax.axis_size("gcol")
    height = nv * planes
    steps = QUARTER // STEP
    pairs = bands * nv
    width = 2 * KG // count
    slots = count * gcol_count
    pieces = KG // PIECE
    share = width // gcol_count
    span = width - share // 128 * 128
    bf16, f32 = jnp.bfloat16, jnp.float32
    left, right, sign = half_plane_tables()
    xtab = plane_table(nv)
    smem = pl.BlockSpec(memory_space=pltpu.SMEM)
    hbm = pl.BlockSpec(memory_space=pl.ANY)
    dma = pltpu.SemaphoreType.DMA
    piece = pltpu.VMEM((pieces, 2 * pairs, PIECE), bf16)
    chunk = [
        pltpu.VMEM((bands * height, STEP), bf16),
        pltpu.VMEM((bands * height, STEP), bf16),
        pltpu.VMEM((bands * height, 2 * STEP), bf16),
    ]
    cols, rows = pl.pallas_call(
        chi_kernel,
        out_shape=(
            jax.ShapeDtypeStruct((slots, pairs, width), bf16),
            jax.ShapeDtypeStruct((slots, pairs, span), bf16),
        ),
        in_specs=[smem] * 3 + [pl.BlockSpec(memory_space=pltpu.VMEM)] + [hbm] * 6,
        out_specs=(hbm, hbm),
        scratch_shapes=[
            pltpu.VMEM((nv, planes, points), bf16),
            pltpu.VMEM((bands, planes, points), bf16),
            pltpu.VMEM(left.shape, f32),
            pltpu.VMEM(right.shape, f32),
            pltpu.VMEM(sign.shape, f32),
            pltpu.VMEM((2, planes, RAD * 4 * nv), f32),
            pltpu.VMEM((QUARTER, 512), bf16),
            pltpu.VMEM((steps, 2 * STEP, 512), bf16),
            *chunk,
            *chunk,
            pltpu.VMEM((bands * height, 512), f32),
            pltpu.VMEM((bands * height, 512), f32),
            pltpu.VMEM((2 * height, RAD * 4 * nv), bf16),
            pltpu.VMEM((RAD * NR, 128), f32),
            pltpu.VMEM((PIECE, 128), f32),
            piece, piece, piece, piece, piece, piece,
            pltpu.VMEM((slots, pairs, width), bf16),
            pltpu.VMEM((slots, pairs, span), bf16),
            pltpu.VMEM((1, KG), jnp.int32),
            pltpu.SMEM((1, KG), jnp.int32),
            dma((8 * steps + 4,)),
            dma((2, pieces)),
            dma((2, pieces)),
            dma((pieces, 2, 2)),
            dma((slots,)),
            dma((width // PIECE, count - 1)),
            dma((count,)),
            dma((count,)),
            dma((count,)),
            dma((1 + 2 * slots,)),
        ],
        compiler_params=pltpu.CompilerParams(
            vmem_limit_bytes=60 * 1024 * 1024, collective_id=0, has_side_effects=True
        ),
    )(
        val_occupation, val_energy, cond_energy, gvectors,
        valence, conduction, left, right, sign, xtab,
    )
    all_pairs = slots * pairs
    prefactor = -1.0 / math.sqrt(all_pairs)
    return product(
        rows.reshape(all_pairs, span), cols.reshape(all_pairs, width), share, prefactor
    )


def either_body(valence, conduction, *rest):
    nv, planes, _ = valence.shape
    count = lax.axis_size("pair")
    width = 2 * KG // count
    fits = (
        count == lax.axis_size("grow")
        and count % 2 == 0
        and lax.axis_size("gcol") == 2
        and planes % 8 == 0
        and conduction.shape[0] == 2
        and 8 * nv == 128
        and width % PIECE == 0
        and width // PIECE % 2 == 1
    )
    return (fast_body if fits else body)(valence, conduction, *rest)


def solution(mesh):
    return jax.shard_map(
        either_body,
        mesh=mesh,
        in_specs=(P(None, "grow", None), P(("pair", "gcol"), "grow", None), P(), P(), P(), P()),
        out_specs=P(("pair", "gcol"), "grow"),
        check_vma=False,
    )
```

time: 59.4 us -> 50.3 us (0.85)
  Pallas kernels: 58.7 us -> 50 us
    pallas_call x1, Pallas kernels: 52.5 us -> 43.9 us  [fast_body(): pl.pallas_call(chi_kernel, out_shape=(jax.ShapeDtypeStruct((slots, pairs,...]
where the time goes in v1:
time: 50.3 us; the launch traced here: 50 us
  Pallas kernels  50 us (99%)
    pallas_call x1, Pallas kernels, fast_body(): pl.pallas_call(chi_kernel, out_shape=(jax.ShapeDtypeStruct((slots, pairs,...  43.9 us
    pallas_call x1, Pallas kernels, product(): pl.pallas_call(functools.partial(product_kernel, prefactor), out_shape=ja...  6.09 us

profile of v1, /device:TPU:27, one launch (start us, length us, event | category | flops | bytes accessed | tf_op | source)
XLA Modules:
  0.0 50.0 jit_solution(16755781071299025873)
XLA Ops:
  0.0 43.9 %shard_map.100 = (bf16[8,32,1920]{2,1,0:T(8,128)(2,1)}, bf16[8,32,1024]{2,1,0:T(8,128)(2,1)}) custom-call(s32[16]{0:T(128)} %occ.1, f32[16]{0:T(128)} %val_e.1, f32[16]{0:T(128)} %cond_e.1, s32[3,3840]{1,0:T(4,128)} %gvec.1, bf16[16,24,9216]{2,1,0:T(8,128)(2,1)} %val.1, bf16[2,24,9216]{2,1,0:T(8,128)(2,1)} %cond.1, f32[2,24,1024]{2,1,0:T(8,128)} %constant.8.clone.left, ...), custom_call_target="tpu_custom_call" | custom-call | tf_op jit(solution)/shard_map/pallas_call | solution.py:578
  43.9 6.1 %shard_map.101 = f32[960,1920]{1,0:T(8,128)} custom-call(bf16[256,1024]{1,0:T(8,128)(2,1)} %bitcast.3, bf16[256,1920]{1,0:T(8,128)(2,1)} %bitcast.2), custom_call_target="tpu_custom_call" | custom-call | tf_op jit(solution)/shard_map/pallas_call | solution.py:540

commit v2 on v1

--- a/solution.py
+++ b/solution.py
@@ -90,14 +90,16 @@
 EXT = 2 * RAD + 1
 QUARTER = N * N // 4
 STEP = 8 * N
+TILE = 256
 CLASSES = ((0, 4, 8, 12), (2, 6, 10), (1, 3, 5, 7, 9, 11))
 WIDTHS = (128, 128, 256)
 ROWS = (104, 80, 152)
 STARTS = (0, 104, 184)
 NR = 336
 TALL = (112, 80, 160)
-PIECE = 384
-LAG = 3
+PIECE = 128
+UNIT = 2
+LAG = 4
 
 
 def half_plane_tables():
@@ -150,8 +152,7 @@
 def chi_kernel(
     occ, val_e, cond_e, gvec, val, cond, left, right, sign, xtab,
     cols_out, rows_out,
-    vbuf, cbuf, leftv, rightv, signv, xv, tabs_e, tabs_o,
-    ee0, eo0, od0, ee1, eo1, od1, acc_e, acc_o, xmat, sec, got,
+    orbitals, leftv, rightv, signv, xv, tabs, folded, acc, xmat, sec, got,
     part, rin, lin, rout, lout, tot, cols, rows, index, idx,
     loads, chain_send, chain_recv, row_send, row_recv, col_send, col_recv,
     over_send, over_recv, outs,
@@ -165,12 +166,12 @@
     half = lanes // 2
     steps = QUARTER // STEP
     pieces = part.shape[0]
+    units = pieces // UNIT
     slots, _, width = cols.shape
     count = slots // 2
     per = width // PIECE
     middle = per // 2
     span = rows.shape[2]
-    low = width - span
     p, g, c = lax.axis_index("pair"), lax.axis_index("grow"), lax.axis_index("gcol")
     me = p * 2 + c
     turn = lambda at, k: lax.rem(at + k, count)
@@ -182,7 +183,7 @@
         )
 
     table_loads = [
-        pltpu.make_async_copy(a, b, loads.at[8 * steps + i])
+        pltpu.make_async_copy(a, b, loads.at[steps + i])
         for i, (a, b) in enumerate(
             (
                 (left, leftv),
@@ -197,21 +198,12 @@
         group = []
         for q in range(4):
             at = pl.ds(q * QUARTER + s * STEP, STEP)
-            for u, (a, b) in enumerate(((cond, cbuf), (val, vbuf))):
-                group.append(
-                    pltpu.make_async_copy(
-                        a.at[:, :, at], b.at[:, :, at], loads.at[8 * s + 2 * q + u]
-                    )
-                )
+            for a, first in ((cond, nv), (val, 0)):
+                b = orbitals.at[pl.ds(first, a.shape[0]), :, at]
+                group.append(pltpu.make_async_copy(a.at[:, :, at], b, loads.at[s]))
         step_loads.append(group)
-    for copy in table_loads[:3]:
+    for copy in table_loads[:3] + sum(step_loads, []) + table_loads[3:]:
         copy.start()
-    for copy in step_loads[0]:
-        copy.start()
-    table_loads[3].start()
-    for group in step_loads[1:]:
-        for copy in group:
-            copy.start()
 
     barrier = pltpu.get_barrier_semaphore()
     pl.semaphore_signal(barrier, inc=1, device_id=(p, g, 1 - c))
@@ -228,63 +220,50 @@
         copy.wait()
 
     def table_rows(y, carry):
-        l1 = leftv[0, pl.ds(y, 1), :]
-        l2 = leftv[1, pl.ds(y, 1), :]
+        l1, l2 = leftv[0, pl.ds(y, 1), :], leftv[1, pl.ds(y, 1), :]
+        at = pl.ds(pl.multiple_of(y * N, 32), N)
         full = l1 * rightv[0] + l2 * rightv[1]
-        w = WIDTHS[2]
-        odd_p, odd_q = full[:, 512 : 512 + w], full[:, 512 + w :]
-        tabs_e[pl.ds(pl.multiple_of(y * N, 32), N), :] = full[:, 0:512].astype(bf16)
-        s = y // (STEP // N)
-        at = pl.multiple_of((y - s * (STEP // N)) * N, 32)
-        tabs_o[s, pl.ds(at, N), 0:w] = odd_p.astype(bf16)
-        tabs_o[s, pl.ds(at, N), w:] = odd_q.astype(bf16)
-        tabs_o[s, pl.ds(STEP + at, N), 0:w] = (odd_q * (0.0 - signv[...])).astype(bf16)
-        tabs_o[s, pl.ds(STEP + at, N), w:] = (odd_p * signv[...]).astype(bf16)
+        odd_p, odd_q = full[:, 2 * TILE : 3 * TILE], full[:, 3 * TILE :]
+        tiles = (
+            full[:, 0:TILE], full[:, TILE : 2 * TILE],
+            odd_p, odd_q * (0.0 - signv[...]), odd_q, odd_p * signv[...],
+        )
+        for i, tile in enumerate(tiles):
+            tabs[i, at, :] = tile.astype(bf16)
         return carry
 
     lax.fori_loop(0, QUARTER // N, table_rows, 0)
 
-    def products(s, ee, eo, od):
-        for copy in step_loads[s]:
-            copy.wait()
+    def ready(s):
+        whole = orbitals.at[:, :, pl.ds(0, 4 * STEP)]
+        pltpu.make_async_copy(whole, whole, loads.at[s]).wait()
+
+    def products(i, carry):
+        at = [pl.ds(pl.multiple_of(q * QUARTER + i * TILE, TILE), TILE) for q in range(4)]
+        here = pl.ds(pl.multiple_of(i * TILE, TILE), TILE)
         for b in range(bands):
-            for m in range(STEP // lanes):
-                at = [pl.ds(q * QUARTER + s * STEP + m * lanes, lanes) for q in range(4)]
-                here = slice(m * lanes, (m + 1) * lanes)
-                there = slice(STEP + m * lanes, STEP + (m + 1) * lanes)
-                cs = [cbuf[b, :, q].astype(f32)[None] for q in at]
-                for v in range(0, nv, 2):
-                    d0, d1, d2, d3 = [
-                        (vbuf[v : v + 2, :, q].astype(f32) * u).reshape(2 * planes, lanes)
-                        for q, u in zip(at, cs)
-                    ]
+            for x in range(0, planes, 8):
+                cs = [orbitals[nv + b, x : x + 8, q] for q in at]
+                for v in range(nv):
+                    d0, d1, d2, d3 = [orbitals[v, x : x + 8, q] * u for q, u in zip(at, cs)]
                     e0, e1 = d0 + d2, d1 + d3
-                    row = b * height + v * planes
-                    where = slice(row, row + 2 * planes)
-                    ee[where, here] = (e0 + e1).astype(bf16)
-                    eo[where, here] = (e0 - e1).astype(bf16)
-                    od[where, here] = (d0 - d2).astype(bf16)
-                    od[where, there] = (d1 - d3).astype(bf16)
-
-    def multiply(s, ee, eo, od):
-        at = slice(s * STEP, (s + 1) * STEP)
-        parts = (
-            (acc_e, slice(0, 256), jnp.dot(ee[...], tabs_e[at, 0:256], preferred_element_type=f32)),
-            (acc_e, slice(256, 512), jnp.dot(eo[...], tabs_e[at, 256:512], preferred_element_type=f32)),
-            (acc_o, slice(0, 512), jnp.dot(od[...], tabs_o[s], preferred_element_type=f32)),
-        )
-        for acc, where, value in parts:
-            if s:
-                acc[:, where] += value
-            else:
-                acc[:, where] = value
-
-    sets = ((ee0, eo0, od0), (ee1, eo1, od1))
-    products(0, *sets[0])
+                    row = b * height + v * planes + x
+                    where = slice(row, row + 8)
+                    folded[0, where, here] = e0 + e1
+                    folded[1, where, here] = e0 - e1
+                    folded[2, where, here] = d0 - d2
+                    folded[3, where, here] = d1 - d3
+        return carry
+
     for s in range(steps):
-        if s + 1 < steps:
-            products(s + 1, *sets[(s + 1) % 2])
-        multiply(s, *sets[s % 2])
+        ready(s)
+        lax.fori_loop(s * STEP // TILE, (s + 1) * STEP // TILE, products, 0)
+
+    dot = lambda i, j: jnp.dot(folded[i], tabs[j], preferred_element_type=f32)
+    acc[0] = dot(0, 0)
+    acc[1] = dot(1, 1)
+    acc[2] = dot(2, 2) + dot(3, 3)
+    acc[3] = dot(2, 4) + dot(3, 5)
 
     table_loads[3].wait()
     own = lax.broadcasted_iota(jnp.int32, (1, RAD * 4 * nv), 1) % nv
@@ -311,16 +290,17 @@
     ]
     lower = lane < half
     groups = (
-        (acc_e, 0, 128, TALL[0], ROWS[0], STARTS[0]),
-        (acc_e, 256, 128, TALL[1], ROWS[1], STARTS[1]),
-        (acc_o, 0, 256, TALL[2], ROWS[2], STARTS[2]),
-    )
-    for acc, base, w, tall, size, start in groups:
+        ((0,), (0,), (0, 128), 128, TALL[0], ROWS[0], STARTS[0]),
+        ((1,), (1,), (0, 128), 128, TALL[1], ROWS[1], STARTS[1]),
+        ((2,), (3,), (0, 0), 256, TALL[2], ROWS[2], STARTS[2]),
+    )
+    for first_of, second_of, bases, size_of, tall, size, start in groups:
         summed = []
         for b in range(bands):
             at = slice(b * height, (b + 1) * height)
             turned = [
-                acc[at, base + h * w : base + (h + 1) * w].astype(bf16).T[0:tall] for h in range(2)
+                sum(acc[i, at, base : base + size_of] for i in which).astype(bf16).T[0:tall]
+                for which, base in zip((first_of, second_of), bases)
             ]
             summed.append(
                 jnp.dot(jnp.concatenate(turned, 1), xmat[...], preferred_element_type=f32)
@@ -338,10 +318,10 @@
     pl.semaphore_wait(barrier, 1 + 3 * (count - 1))
 
     def pick(n):
+        at = pl.ds(pl.multiple_of(n * PIECE, PIECE), PIECE)
         for u in range(PIECE):
             got[u : u + 1, :] = sec[pl.ds(idx[0, n * PIECE + u], 1), :]
         turned = got[...].T
-        at = slice(n * PIECE, (n + 1) * PIECE)
         odd = ((gvec[0:1, at] - 1) & 1) == 1
         flip = gvec[1:2, at] < 0
         top, bottom = turned[0:half], turned[half:lanes]
@@ -351,19 +331,21 @@
             part[n, pairs + b * nv : pairs + (b + 1) * nv, :] = chosen[nv : 2 * nv]
 
     def right_copy(src, t):
+        at = pl.ds(t * UNIT, UNIT)
         return remote(
-            src.at[t], rin.at[t], chain_send.at[0, t], chain_recv.at[0, t],
+            src.at[at], rin.at[at], chain_send.at[0], chain_recv.at[0, t],
             (p, jnp.minimum(g + 1, count - 1), c),
         )
 
     def left_copy(src, t):
+        at = pl.ds(t * UNIT, UNIT)
         return remote(
-            src.at[t], lin.at[t], chain_send.at[1, t], chain_recv.at[1, t],
+            src.at[at], lin.at[at], chain_send.at[1], chain_recv.at[1, t],
             (p, jnp.maximum(g - 1, 0), c),
         )
 
     def chain(t, make, came, passed, first, last):
-        @pl.when((t >= 0) & (t < pieces))
+        @pl.when((t >= 0) & (t < units))
         def _():
             @pl.when(first)
             def _():
@@ -375,107 +357,120 @@
 
                 @pl.when(jnp.logical_not(last))
                 def _():
-                    passed[t] = (part[t].astype(f32) + came[t].astype(f32)).astype(bf16)
+                    at = pl.ds(t * UNIT, UNIT)
+                    passed[at] = (part[at].astype(f32) + came[at].astype(f32)).astype(bf16)
                     make(passed, t).start()
 
-    def row_copy(t, r, b, d, lo, wide, to):
+    def row_copy(t, r, b, d, j):
+        at = pl.ds(pl.multiple_of(j * PIECE, PIECE), PIECE)
         return remote(
-            tot.at[t, pl.ds(r * pairs, pairs), pl.ds(lo, wide)],
-            rows.at[me, :, pl.ds(to, wide)],
-            row_send.at[t, r, d], row_recv.at[me], (b, g, d),
-        )
-
-    def put(t, r, b, d, lo, wide, to):
+            tot.at[t, pl.ds(r * pairs, pairs), :], rows.at[me, :, at],
+            row_send.at[0], row_recv.at[me], (b, g, d),
+        )
+
+    def put(t, r, b, d, j):
         here = (b == p) & (d == c)
 
         @pl.when(here)
         def _():
-            rows[me, :, pl.ds(to, wide)] = tot[t, r * pairs : (r + 1) * pairs, lo : lo + wide]
+            at = pl.ds(pl.multiple_of(j * PIECE, PIECE), PIECE)
+            rows[me, :, at] = tot[t, r * pairs : (r + 1) * pairs, :]
 
         @pl.when(jnp.logical_not(here))
         def _():
-            row_copy(t, r, b, d, lo, wide, to).start()
+            row_copy(t, r, b, d, j).start()
 
     def col_copy(t, r, j, k):
         at = pl.ds(pl.multiple_of(j * PIECE, 128), PIECE)
         return remote(
             tot.at[t, pl.ds(r * pairs, pairs), :], cols.at[me, :, at],
-            col_send.at[j, k - 1], col_recv.at[p], (turn(p, k), g, c),
-        )
-
-    def finish(t):
-        @pl.when((t >= 0) & (t < pieces))
+            col_send.at[0], col_recv.at[p], (turn(p, k), g, c),
+        )
+
+    def deliver(t):
+        h = t // per
+        j = t - h * per
+        for r in range(2):
+            b = h + r * (count // 2)
+
+            @pl.when(j <= middle)
+            def _():
+                put(t, r, b, 0, j)
+
+            @pl.when(j >= middle)
+            def _():
+                put(t, r, b, 1, j - middle)
+
+            @pl.when(b == g)
+            def _():
+                at = pl.ds(pl.multiple_of(j * PIECE, 128), PIECE)
+                cols[me, :, at] = tot[t, r * pairs : (r + 1) * pairs, :]
+                for k in range(1, count):
+                    col_copy(t, r, j, k).start()
+
+    def finish(u):
+        @pl.when((u >= 0) & (u < units))
         def _():
-            mine = lambda: part[t].astype(f32)
+            at = pl.ds(u * UNIT, UNIT)
+            mine = lambda: part[at].astype(f32)
 
             @pl.when(g == 0)
             def _():
-                tot[t] = (mine() + lin[t].astype(f32)).astype(bf16)
+                tot[at] = (mine() + lin[at].astype(f32)).astype(bf16)
 
             @pl.when(g == count - 1)
             def _():
-                tot[t] = (mine() + rin[t].astype(f32)).astype(bf16)
+                tot[at] = (mine() + rin[at].astype(f32)).astype(bf16)
 
             @pl.when((g > 0) & (g < count - 1))
             def _():
-                tot[t] = (mine() + rin[t].astype(f32) + lin[t].astype(f32)).astype(bf16)
-
-            h = t // per
-            j = t - h * per
-            for r in range(2):
-                b = h + r * (count // 2)
-
-                @pl.when(j < middle)
-                def _():
-                    put(t, r, b, 0, 0, PIECE, pl.multiple_of(j * PIECE, 128))
-
-                @pl.when(j > middle)
-                def _():
-                    put(t, r, b, 1, 0, PIECE, pl.multiple_of(j * PIECE - low, 128))
-
-                @pl.when(j == middle)
-                def _():
-                    put(t, r, b, 0, 0, span - middle * PIECE, middle * PIECE)
-                    put(t, r, b, 1, low - middle * PIECE, (middle + 1) * PIECE - low, 0)
-
-                @pl.when(b == g)
-                def _():
-                    at = pl.ds(pl.multiple_of(j * PIECE, 128), PIECE)
-                    cols[me, :, at] = tot[t, r * pairs : (r + 1) * pairs, :]
-                    for k in range(1, count):
-                        col_copy(t, r, j, k).start()
-
-    for n in range(pieces + LAG * (count - 1)):
-        if n < pieces:
-            pick(n)
+                tot[at] = (mine() + rin[at].astype(f32) + lin[at].astype(f32)).astype(bf16)
+
+            for i in range(UNIT):
+                deliver(u * UNIT + i)
+
+    def serve(n):
         to_right = n - g * LAG
         to_left = n - (count - 1 - g) * LAG
         chain(to_right, right_copy, rin, rout, g == 0, g == count - 1)
         chain(to_left, left_copy, lin, lout, g == count - 1, g == 0)
         finish(jnp.minimum(to_right, to_left))
 
+    def early(n, carry):
+        for i in range(UNIT):
+            pick(n * UNIT + i)
+        serve(n)
+        return carry
+
+    def late(n, carry):
+        serve(n)
+        return carry
+
+    lax.fori_loop(0, units, early, 0)
+    lax.fori_loop(units, units + LAG * (count - 1), late, 0)
+
     def over(q, core):
         slot = q * 2 + core
         return remote(
-            cols.at[slot], cols.at[slot], over_send.at[q], over_recv.at[q], (p, g, 1 - c)
+            cols.at[slot], cols.at[slot], over_send.at[0], over_recv.at[q], (p, g, 1 - c)
         )
 
     def out_copy(ref, dst, slot, which):
-        return pltpu.make_async_copy(ref.at[slot], dst.at[slot], outs.at[1 + which * slots + slot])
+        return pltpu.make_async_copy(ref.at[slot], dst.at[slot], outs.at[1 + which])
 
     over(p, c).start()
     out_copy(cols, cols_out, me, 0).start()
     for k in range(1, count):
         q = turn(p, k)
         at = q * 2 + c
-        remote(cols.at[at], cols.at[at], col_send.at[0, 0], col_recv.at[q], (q, g, c)).wait_recv()
+        remote(cols.at[at], cols.at[at], col_send.at[0], col_recv.at[q], (q, g, c)).wait_recv()
         over(q, c).start()
         out_copy(cols, cols_out, at, 0).start()
     for slot in range(slots):
         @pl.when(slot != me)
         def _():
             remote(
-                rows.at[slot], rows.at[slot], row_send.at[0, 0, 0], row_recv.at[slot],
+                rows.at[slot], rows.at[slot], row_send.at[0], row_recv.at[slot],
                 (slot // 2, g, slot % 2),
             ).wait_recv()
 
@@ -485,39 +480,22 @@
         over(q, 1 - c).wait_recv()
         out_copy(cols, cols_out, q * 2 + 1 - c, 0).start()
 
-    for t in range(pieces):
-        @pl.when(g < count - 1)
-        def _():
-            right_copy(part, t).wait_send()
-
-        @pl.when(g > 0)
-        def _():
-            left_copy(part, t).wait_send()
-
-        h, j = t // per, t % per
-        for r in range(2):
-            b = h + r * (count // 2)
-            for d in range(2):
-                if (j < middle and d == 1) or (j > middle and d == 0):
-                    continue
-                wide = PIECE
-                if j == middle:
-                    wide = (middle + 1) * PIECE - low if d else span - middle * PIECE
-
-                @pl.when(jnp.logical_not((p == b) & (c == d)))
-                def _():
-                    row_copy(t, r, b, d, 0, wide, 0).wait_send()
-
-            @pl.when(g == b)
-            def _():
-                for k in range(1, count):
-                    col_copy(t, r, j, k).wait_send()
-
-    for q in range(count):
-        over(q, c).wait_send()
-    for slot in range(slots):
-        out_copy(cols, cols_out, slot, 0).wait()
-        out_copy(rows, rows_out, slot, 1).wait()
+    def sent(ref, sem):
+        remote(ref, ref, sem, row_recv.at[0], (p, g, 1 - c)).wait_send()
+
+    @pl.when(g < count - 1)
+    def _():
+        sent(part, chain_send.at[0])
+
+    @pl.when(g > 0)
+    def _():
+        sent(part, chain_send.at[1])
+
+    sent(rows.at[pl.ds(0, slots - 1)], row_send.at[0])
+    sent(cols.at[pl.ds(0, count - 1)], col_send.at[0])
+    sent(cols.at[pl.ds(0, count)], over_send.at[0])
+    pltpu.make_async_copy(cols, cols_out, outs.at[1]).wait()
+    pltpu.make_async_copy(rows, rows_out, outs.at[2]).wait()
 
 
 def product_kernel(prefactor, rows, cols, out, turned):
@@ -570,11 +548,6 @@
     hbm = pl.BlockSpec(memory_space=pl.ANY)
     dma = pltpu.SemaphoreType.DMA
     piece = pltpu.VMEM((pieces, 2 * pairs, PIECE), bf16)
-    chunk = [
-        pltpu.VMEM((bands * height, STEP), bf16),
-        pltpu.VMEM((bands * height, STEP), bf16),
-        pltpu.VMEM((bands * height, 2 * STEP), bf16),
-    ]
     cols, rows = pl.pallas_call(
         chi_kernel,
         out_shape=(
@@ -584,18 +557,14 @@
         in_specs=[smem] * 3 + [pl.BlockSpec(memory_space=pltpu.VMEM)] + [hbm] * 6,
         out_specs=(hbm, hbm),
         scratch_shapes=[
-            pltpu.VMEM((nv, planes, points), bf16),
-            pltpu.VMEM((bands, planes, points), bf16),
+            pltpu.VMEM((nv + bands, planes, points), bf16),
             pltpu.VMEM(left.shape, f32),
             pltpu.VMEM(right.shape, f32),
             pltpu.VMEM(sign.shape, f32),
             pltpu.VMEM((2, planes, RAD * 4 * nv), f32),
-            pltpu.VMEM((QUARTER, 512), bf16),
-            pltpu.VMEM((steps, 2 * STEP, 512), bf16),
-            *chunk,
-            *chunk,
-            pltpu.VMEM((bands * height, 512), f32),
-            pltpu.VMEM((bands * height, 512), f32),
+            pltpu.VMEM((6, QUARTER, TILE), bf16),
+            pltpu.VMEM((4, bands * height, QUARTER), bf16),
+            pltpu.VMEM((4, bands * height, TILE), f32),
             pltpu.VMEM((2 * height, RAD * 4 * nv), bf16),
             pltpu.VMEM((RAD * NR, 128), f32),
             pltpu.VMEM((PIECE, 128), f32),
@@ -604,16 +573,16 @@
             pltpu.VMEM((slots, pairs, span), bf16),
             pltpu.VMEM((1, KG), jnp.int32),
             pltpu.SMEM((1, KG), jnp.int32),
-            dma((8 * steps + 4,)),
-            dma((2, pieces)),
-            dma((2, pieces)),
-            dma((pieces, 2, 2)),
+            dma((steps + 4,)),
+            dma((2,)),
+            dma((2, pieces // UNIT)),
+            dma((1,)),
             dma((slots,)),
-            dma((width // PIECE, count - 1)),
+            dma((1,)),
             dma((count,)),
+            dma((1,)),
             dma((count,)),
-            dma((count,)),
-            dma((1 + 2 * slots,)),
+            dma((3,)),
         ],
         compiler_params=pltpu.CompilerParams(
             vmem_limit_bytes=60 * 1024 * 1024, collective_id=0, has_side_effects=True
@@ -642,6 +611,7 @@
         and 8 * nv == 128
         and width % PIECE == 0
         and width // PIECE % 2 == 1
+        and KG // PIECE % UNIT == 0
     )
     return (fast_body if fits else body)(valence, conduction, *rest)
 

time: 50.3 us -> 47.9 us (0.952)
  Pallas kernels: 50 us -> 47.7 us
    pallas_call x1, Pallas kernels: 43.9 us -> 41.6 us  [fast_body(): pl.pallas_call(chi_kernel, out_shape=(jax.ShapeDtypeStruct((slots, pairs,...]
where the time goes in v2:
time: 47.9 us; the launch traced here: 47.7 us
  Pallas kernels  47.7 us (100%)
    pallas_call x1, Pallas kernels, fast_body(): pl.pallas_call(chi_kernel, out_shape=(jax.ShapeDtypeStruct((slots, pairs,...  41.6 us
    pallas_call x1, Pallas kernels, product(): pl.pallas_call(functools.partial(product_kernel, prefactor), out_shape=ja...  6.09 us

profile of v2, /device:TPU:27, one launch (start us, length us, event | category | flops | bytes accessed | tf_op | source)
XLA Modules:
  0.0 47.7 jit_solution(13912761204036599026)
XLA Ops:
  0.0 41.6 %shard_map.100 = (bf16[8,32,1920]{2,1,0:T(8,128)(2,1)}, bf16[8,32,1024]{2,1,0:T(8,128)(2,1)}) custom-call(s32[16]{0:T(128)} %occ.1, f32[16]{0:T(128)} %val_e.1, f32[16]{0:T(128)} %cond_e.1, s32[3,3840]{1,0:T(4,128)} %gvec.1, bf16[16,24,9216]{2,1,0:T(8,128)(2,1)} %val.1, bf16[2,24,9216]{2,1,0:T(8,128)(2,1)} %cond.1, f32[2,24,1024]{2,1,0:T(8,128)} %constant.8.clone.left, ...), custom_call_target="tpu_custom_call" | custom-call | tf_op jit(solution)/shard_map/pallas_call | solution.py:551
  41.6 6.1 %shard_map.101 = f32[960,1920]{1,0:T(8,128)} custom-call(bf16[256,1024]{1,0:T(8,128)(2,1)} %bitcast.3, bf16[256,1920]{1,0:T(8,128)(2,1)} %bitcast.2), custom_call_target="tpu_custom_call" | custom-call | tf_op jit(solution)/shard_map/pallas_call | solution.py:518

commit v3 on v2

--- a/solution.py
+++ b/solution.py
@@ -150,10 +150,10 @@
 
 
 def chi_kernel(
-    occ, val_e, cond_e, gvec, val, cond, left, right, sign, xtab,
-    cols_out, rows_out,
-    orbitals, leftv, rightv, signv, xv, tabs, folded, acc, xmat, sec, got,
-    part, rin, lin, rout, lout, tot, cols, rows, index, idx,
+    occ_in, val_in, cond_in, gvec_in, val, cond, left, right, sign, xtab,
+    cols, rows,
+    occ, val_e, cond_e, gvec, orbitals, leftv, rightv, signv, xv, tabs, folded, acc, xmat, sec, got,
+    part, rin, lin, rout, lout, tot, index, idx,
     loads, chain_send, chain_recv, row_send, row_recv, col_send, col_recv,
     over_send, over_recv, outs,
 ):
@@ -189,7 +189,11 @@
                 (left, leftv),
                 (right, rightv),
                 (sign, signv),
+                (gvec_in, gvec),
                 (xtab.at[:, pl.ds(pl.multiple_of(g * planes, 8), planes), :], xv),
+                (occ_in, occ),
+                (val_in, val_e),
+                (cond_in, cond_e),
             )
         )
     ]
@@ -202,7 +206,7 @@
                 b = orbitals.at[pl.ds(first, a.shape[0]), :, at]
                 group.append(pltpu.make_async_copy(a.at[:, :, at], b, loads.at[s]))
         step_loads.append(group)
-    for copy in table_loads[:3] + sum(step_loads, []) + table_loads[3:]:
+    for copy in table_loads[:4] + sum(step_loads, []) + table_loads[4:]:
         copy.start()
 
     barrier = pltpu.get_barrier_semaphore()
@@ -212,12 +216,11 @@
             pl.semaphore_signal(barrier, inc=1, device_id=(turn(p, k), g, d))
         pl.semaphore_signal(barrier, inc=1, device_id=(p, turn(g, k), c))
 
+    for copy in table_loads[:4]:
+        copy.wait()
     index[...] = row_index(gvec[0:1, :], gvec[1:2, :], gvec[2:3, :])
     index_copy = pltpu.make_async_copy(index, idx, outs.at[0])
     index_copy.start()
-
-    for copy in table_loads[:3]:
-        copy.wait()
 
     def table_rows(y, carry):
         l1, l2 = leftv[0, pl.ds(y, 1), :], leftv[1, pl.ds(y, 1), :]
@@ -265,7 +268,8 @@
     acc[2] = dot(2, 2) + dot(3, 3)
     acc[3] = dot(2, 4) + dot(3, 5)
 
-    table_loads[3].wait()
+    for copy in table_loads[4:]:
+        copy.wait()
     own = lax.broadcasted_iota(jnp.int32, (1, RAD * 4 * nv), 1) % nv
 
     def place(v, carry):
@@ -455,17 +459,12 @@
             cols.at[slot], cols.at[slot], over_send.at[0], over_recv.at[q], (p, g, 1 - c)
         )
 
-    def out_copy(ref, dst, slot, which):
-        return pltpu.make_async_copy(ref.at[slot], dst.at[slot], outs.at[1 + which])
-
     over(p, c).start()
-    out_copy(cols, cols_out, me, 0).start()
     for k in range(1, count):
         q = turn(p, k)
         at = q * 2 + c
         remote(cols.at[at], cols.at[at], col_send.at[0], col_recv.at[q], (q, g, c)).wait_recv()
         over(q, c).start()
-        out_copy(cols, cols_out, at, 0).start()
     for slot in range(slots):
         @pl.when(slot != me)
         def _():
@@ -474,11 +473,9 @@
                 (slot // 2, g, slot % 2),
             ).wait_recv()
 
-        out_copy(rows, rows_out, slot, 1).start()
     for k in range(count):
         q = turn(p, k)
         over(q, 1 - c).wait_recv()
-        out_copy(cols, cols_out, q * 2 + 1 - c, 0).start()
 
     def sent(ref, sem):
         remote(ref, ref, sem, row_recv.at[0], (p, g, 1 - c)).wait_send()
@@ -494,8 +491,6 @@
     sent(rows.at[pl.ds(0, slots - 1)], row_send.at[0])
     sent(cols.at[pl.ds(0, count - 1)], col_send.at[0])
     sent(cols.at[pl.ds(0, count)], over_send.at[0])
-    pltpu.make_async_copy(cols, cols_out, outs.at[1]).wait()
-    pltpu.make_async_copy(rows, rows_out, outs.at[2]).wait()
 
 
 def product_kernel(prefactor, rows, cols, out, turned):
@@ -514,7 +509,7 @@
 def product(rows, cols, share, prefactor):
     depth, width = cols.shape
     span = rows.shape[1]
-    tile = 384
+    tile = 640
     return pl.pallas_call(
         functools.partial(product_kernel, prefactor),
         out_shape=jax.ShapeDtypeStruct((share, width), jnp.float32),
@@ -525,6 +520,7 @@
         ],
         out_specs=pl.BlockSpec((share, tile), lambda i: (0, i)),
         scratch_shapes=[pltpu.VMEM((span, depth), jnp.bfloat16)],
+        compiler_params=pltpu.CompilerParams(vmem_limit_bytes=24 * 1024 * 1024),
     )(rows, cols)
 
 
@@ -544,19 +540,23 @@
     bf16, f32 = jnp.bfloat16, jnp.float32
     left, right, sign = half_plane_tables()
     xtab = plane_table(nv)
-    smem = pl.BlockSpec(memory_space=pltpu.SMEM)
-    hbm = pl.BlockSpec(memory_space=pl.ANY)
+    hbm = pl.BlockSpec(memory_space=pltpu.HBM)
+    vmem = pl.BlockSpec(memory_space=pltpu.VMEM)
     dma = pltpu.SemaphoreType.DMA
     piece = pltpu.VMEM((pieces, 2 * pairs, PIECE), bf16)
     cols, rows = pl.pallas_call(
         chi_kernel,
         out_shape=(
-            jax.ShapeDtypeStruct((slots, pairs, width), bf16),
-            jax.ShapeDtypeStruct((slots, pairs, span), bf16),
+            pltpu.VMEM((slots, pairs, width), bf16),
+            pltpu.VMEM((slots, pairs, span), bf16),
         ),
-        in_specs=[smem] * 3 + [pl.BlockSpec(memory_space=pltpu.VMEM)] + [hbm] * 6,
-        out_specs=(hbm, hbm),
+        in_specs=[hbm] * 10,
+        out_specs=(vmem, vmem),
         scratch_shapes=[
+            pltpu.SMEM(val_occupation.shape, jnp.int32),
+            pltpu.SMEM(val_energy.shape, f32),
+            pltpu.SMEM(cond_energy.shape, f32),
+            pltpu.VMEM(gvectors.shape, jnp.int32),
             pltpu.VMEM((nv + bands, planes, points), bf16),
             pltpu.VMEM(left.shape, f32),
             pltpu.VMEM(right.shape, f32),
@@ -569,11 +569,9 @@
             pltpu.VMEM((RAD * NR, 128), f32),
             pltpu.VMEM((PIECE, 128), f32),
             piece, piece, piece, piece, piece, piece,
-            pltpu.VMEM((slots, pairs, width), bf16),
-            pltpu.VMEM((slots, pairs, span), bf16),
             pltpu.VMEM((1, KG), jnp.int32),
             pltpu.SMEM((1, KG), jnp.int32),
-            dma((steps + 4,)),
+            dma((steps + 8,)),
             dma((2,)),
             dma((2, pieces // UNIT)),
             dma((1,)),
@@ -582,7 +580,7 @@
             dma((count,)),
             dma((1,)),
             dma((count,)),
-            dma((3,)),
+            dma((1,)),
         ],
         compiler_params=pltpu.CompilerParams(
             vmem_limit_bytes=60 * 1024 * 1024, collective_id=0, has_side_effects=True

time: 47.9 us -> 44.6 us (0.931)
  Pallas kernels: 47.7 us -> 44.4 us
    pallas_call x1, Pallas kernels: 6.09 us -> 4.26 us  [product(): pl.pallas_call(functools.partial(product_kernel, prefactor), out_shape=ja...]
    pallas_call x1, Pallas kernels: 41.6 us -> 40.1 us  [fast_body(): pl.pallas_call(chi_kernel, out_shape=(pltpu.VMEM((slots, pairs, width), b...]
where the time goes in v3:
time: 44.6 us; the launch traced here: 44.4 us
  Pallas kernels  44.4 us (100%)
    pallas_call x1, Pallas kernels, fast_body(): pl.pallas_call(chi_kernel, out_shape=(pltpu.VMEM((slots, pairs, width), b...  40.1 us
    pallas_call x1, Pallas kernels, product(): pl.pallas_call(functools.partial(product_kernel, prefactor), out_shape=ja...  4.26 us

profile of v3, /device:TPU:27, one launch (start us, length us, event | category | flops | bytes accessed | tf_op | source)
XLA Modules:
  0.0 44.4 jit_solution(2186462128533591064)
XLA Ops:
  0.0 40.1 %shard_map.100 = (bf16[8,32,1920]{2,1,0:T(8,128)(2,1)S(1)}, bf16[8,32,1024]{2,1,0:T(8,128)(2,1)S(1)}) custom-call(s32[16]{0:T(128)} %occ_in.1, f32[16]{0:T(128)} %val_in.1, f32[16]{0:T(128)} %cond_in.1, s32[3,3840]{1,0:T(4,128)} %gvec_in.1, bf16[16,24,9216]{2,1,0:T(8,128)(2,1)} %val.1, bf16[2,24,9216]{2,1,0:T(8,128)(2,1)} %cond.1, ...), custom_call_target="tpu_custom_call" | custom-call | tf_op jit(solution)/shard_map/pallas_call | solution.py:547
  40.2 4.3 %shard_map.101 = f32[960,1920]{1,0:T(8,128)} custom-call(bf16[256,1024]{1,0:T(8,128)(2,1)S(1)} %bitcast.3, bf16[256,1920]{1,0:T(8,128)(2,1)S(1)} %bitcast.2), custom_call_target="tpu_custom_call" | custom-call | tf_op jit(solution)/shard_map/pallas_call | solution.py:513

commit v4 on v3

--- a/solution.py
+++ b/solution.py
@@ -98,8 +98,8 @@
 NR = 336
 TALL = (112, 80, 160)
 PIECE = 128
-UNIT = 2
-LAG = 4
+UNIT = 1
+LAG = 6
 
 
 def half_plane_tables():
@@ -493,33 +493,37 @@
     sent(cols.at[pl.ds(0, count)], over_send.at[0])
 
 
-def product_kernel(prefactor, rows, cols, out, turned):
-    share = out.shape[0]
+def product_kernel(prefactor, tile, rows, cols, out, turned, held, sems):
+    share, width = out.shape
     c = lax.axis_index("gcol")
     shift = rows.shape[1] - share
-
-    @pl.when(pl.program_id(0) == 0)
-    def _():
-        turned[...] = rows[...].T
-
+    turned[...] = rows[...].T
     left = turned[pl.ds(pl.multiple_of(c * shift, 16), share), :]
-    out[...] = jnp.dot(left, cols[...], preferred_element_type=jnp.float32) * prefactor
+    copies = []
+    for i, start in enumerate(range(0, width, tile)):
+        at = pl.ds(start, min(tile, width - start))
+        held[:, at] = jnp.dot(left, cols[:, at], preferred_element_type=jnp.float32) * prefactor
+        copies.append(pltpu.make_async_copy(held.at[:, at], out.at[:, at], sems.at[i]))
+        copies[-1].start()
+    for copy in copies:
+        copy.wait()
 
 
 def product(rows, cols, share, prefactor):
     depth, width = cols.shape
     span = rows.shape[1]
-    tile = 640
+    tile = 512
+    vmem = pl.BlockSpec(memory_space=pltpu.VMEM)
     return pl.pallas_call(
-        functools.partial(product_kernel, prefactor),
+        functools.partial(product_kernel, prefactor, tile),
         out_shape=jax.ShapeDtypeStruct((share, width), jnp.float32),
-        grid=(width // tile,),
-        in_specs=[
-            pl.BlockSpec((depth, span), lambda i: (0, 0)),
-            pl.BlockSpec((depth, tile), lambda i: (0, i)),
+        in_specs=[vmem, vmem],
+        out_specs=pl.BlockSpec(memory_space=pltpu.HBM),
+        scratch_shapes=[
+            pltpu.VMEM((span, depth), jnp.bfloat16),
+            pltpu.VMEM((share, width), jnp.float32),
+            pltpu.SemaphoreType.DMA((pl.cdiv(width, tile),)),
         ],
-        out_specs=pl.BlockSpec((share, tile), lambda i: (0, i)),
-        scratch_shapes=[pltpu.VMEM((span, depth), jnp.bfloat16)],
         compiler_params=pltpu.CompilerParams(vmem_limit_bytes=24 * 1024 * 1024),
     )(rows, cols)
 

time: 44.6 us -> 43.5 us (0.975)
  Pallas kernels: 44.4 us -> 43.4 us
    pallas_call x1, Pallas kernels: 4.26 us -> 3.64 us  [product(): pl.pallas_call(functools.partial(product_kernel, prefactor, tile), out_sh...]
where the time goes in v4:
time: 43.5 us; the launch traced here: 43.4 us
  Pallas kernels  43.4 us (100%)
    pallas_call x1, Pallas kernels, fast_body(): pl.pallas_call(chi_kernel, out_shape=(pltpu.VMEM((slots, pairs, width), b...  39.7 us
    pallas_call x1, Pallas kernels, product(): pl.pallas_call(functools.partial(product_kernel, prefactor, tile), out_sh...  3.64 us

profile of v4, /device:TPU:27, one launch (start us, length us, event | category | flops | bytes accessed | tf_op | source)
XLA Modules:
  0.0 43.4 jit_solution(4556111023018339115)
XLA Ops:
  0.0 39.7 %shard_map.100 = (bf16[8,32,1920]{2,1,0:T(8,128)(2,1)S(1)}, bf16[8,32,1024]{2,1,0:T(8,128)(2,1)S(1)}) custom-call(s32[16]{0:T(128)} %occ_in.1, f32[16]{0:T(128)} %val_in.1, f32[16]{0:T(128)} %cond_in.1, s32[3,3840]{1,0:T(4,128)} %gvec_in.1, bf16[16,24,9216]{2,1,0:T(8,128)(2,1)} %val.1, bf16[2,24,9216]{2,1,0:T(8,128)(2,1)} %cond.1, ...), custom_call_target="tpu_custom_call" | custom-call | tf_op jit(solution)/shard_map/pallas_call | solution.py:551
  39.8 3.6 %shard_map.101 = f32[960,1920]{1,0:T(8,128)} custom-call(bf16[256,1024]{1,0:T(8,128)(2,1)S(1)} %bitcast.3, bf16[256,1920]{1,0:T(8,128)(2,1)S(1)} %bitcast.2), custom_call_target="tpu_custom_call" | custom-call | tf_op jit(solution)/shard_map/pallas_call | solution.py:517

commit v5 on v4

--- a/solution.py
+++ b/solution.py
@@ -263,10 +263,10 @@
         lax.fori_loop(s * STEP // TILE, (s + 1) * STEP // TILE, products, 0)
 
     dot = lambda i, j: jnp.dot(folded[i], tabs[j], preferred_element_type=f32)
-    acc[0] = dot(0, 0)
-    acc[1] = dot(1, 1)
-    acc[2] = dot(2, 2) + dot(3, 3)
-    acc[3] = dot(2, 4) + dot(3, 5)
+    acc[0] = dot(0, 0).astype(bf16)
+    acc[1] = dot(1, 1).astype(bf16)
+    acc[2] = (dot(2, 2) + dot(3, 3)).astype(bf16)
+    acc[3] = (dot(2, 4) + dot(3, 5)).astype(bf16)
 
     for copy in table_loads[4:]:
         copy.wait()
@@ -294,16 +294,16 @@
     ]
     lower = lane < half
     groups = (
-        ((0,), (0,), (0, 128), 128, TALL[0], ROWS[0], STARTS[0]),
-        ((1,), (1,), (0, 128), 128, TALL[1], ROWS[1], STARTS[1]),
-        ((2,), (3,), (0, 0), 256, TALL[2], ROWS[2], STARTS[2]),
+        (0, 0, (0, 128), 128, TALL[0], ROWS[0], STARTS[0]),
+        (1, 1, (0, 128), 128, TALL[1], ROWS[1], STARTS[1]),
+        (2, 3, (0, 0), 256, TALL[2], ROWS[2], STARTS[2]),
     )
     for first_of, second_of, bases, size_of, tall, size, start in groups:
         summed = []
         for b in range(bands):
             at = slice(b * height, (b + 1) * height)
             turned = [
-                sum(acc[i, at, base : base + size_of] for i in which).astype(bf16).T[0:tall]
+                acc[which, at, base : base + size_of].T[0:tall]
                 for which, base in zip((first_of, second_of), bases)
             ]
             summed.append(
@@ -568,7 +568,7 @@
             pltpu.VMEM((2, planes, RAD * 4 * nv), f32),
             pltpu.VMEM((6, QUARTER, TILE), bf16),
             pltpu.VMEM((4, bands * height, QUARTER), bf16),
-            pltpu.VMEM((4, bands * height, TILE), f32),
+            pltpu.VMEM((4, bands * height, TILE), bf16),
             pltpu.VMEM((2 * height, RAD * 4 * nv), bf16),
             pltpu.VMEM((RAD * NR, 128), f32),
             pltpu.VMEM((PIECE, 128), f32),

time: 43.5 us -> 43.5 us (level)
  no operation moved by 1% of the time
where the time goes in v5:
time: 43.5 us; the launch traced here: 43.4 us
  Pallas kernels  43.4 us (100%)
    pallas_call x1, Pallas kernels, fast_body(): pl.pallas_call(chi_kernel, out_shape=(pltpu.VMEM((slots, pairs, width), b...  39.8 us
    pallas_call x1, Pallas kernels, product(): pl.pallas_call(functools.partial(product_kernel, prefactor, tile), out_sh...  3.64 us

profile of v5, /device:TPU:27, one launch (start us, length us, event | category | flops | bytes accessed | tf_op | source)
XLA Modules:
  0.0 43.4 jit_solution(1845301152739435952)
XLA Ops:
  0.0 39.8 %shard_map.100 = (bf16[8,32,1920]{2,1,0:T(8,128)(2,1)S(1)}, bf16[8,32,1024]{2,1,0:T(8,128)(2,1)S(1)}) custom-call(s32[16]{0:T(128)} %occ_in.1, f32[16]{0:T(128)} %val_in.1, f32[16]{0:T(128)} %cond_in.1, s32[3,3840]{1,0:T(4,128)} %gvec_in.1, bf16[16,24,9216]{2,1,0:T(8,128)(2,1)} %val.1, bf16[2,24,9216]{2,1,0:T(8,128)(2,1)} %cond.1, ...), custom_call_target="tpu_custom_call" | custom-call | tf_op jit(solution)/shard_map/pallas_call | solution.py:551
  39.8 3.6 %shard_map.101 = f32[960,1920]{1,0:T(8,128)} custom-call(bf16[256,1024]{1,0:T(8,128)(2,1)S(1)} %bitcast.3, bf16[256,1920]{1,0:T(8,128)(2,1)S(1)} %bitcast.2), custom_call_target="tpu_custom_call" | custom-call | tf_op jit(solution)/shard_map/pallas_call | solution.py:517
